TPU v7x, 32 devices: a whole 2x2x4 slice. The times are simulated.
32 devices in a mesh: blk: 16 (over z, y, x), row: 2 (over core).
Axes of the slice: x: 2, y: 2, z: 4, core: 2. Of those that a mesh axis runs over, the one named last changes fastest.
Arguments:
- genotypes: bfloat16 [128, 16, 2048], P('blk', None, 'row'), may hold values from 0 to 2
- assignment: int32 [16], replicated, may hold values from 0 to 15, each once
- snp_counts: int32 [16], replicated, may hold values from 1024 to 2048, as said below
- basis: float32 [16, 64, 2048], P('blk', None, 'row'), may hold values from -6 to 6
Outputs:
- image: float32 [16, 64, 2048], P('blk', None, 'row')
- new_basis: float32 [16, 64, 2048], P('blk', None, 'row')
- factor: float32 [16, 64, 64], P('blk')
Inputs may be any that keep to these rules, and one draw needn't show every extreme that they name: `assignment`: each block number appears exactly once. `snp_counts`: A block's SNPs fill its leading slots.
All inputs are finite; a program needn't handle non-finite values.
Results may differ from a plain program's by a relative error of at most 0.0021.
Values may be sent and summed in bfloat16 or wider, within the bound.
No kernel may reach another device: no remote copies, remote signals or barrier semaphores. Data moves between devices by JAX's collectives and lax.ppermute only.
A program may use at most 64 MiB of HBM per device.

v0:
```python
import jax
import jax.numpy as jnp
from jax import lax
from jax.sharding import PartitionSpec as P

epsilon = 1e-05
shrink_weight = 0.5


def body(genotypes, assignment, snp_counts, basis):
    ordered = jnp.take(genotypes, assignment, axis=1)
    regrouped = lax.all_to_all(ordered, "blk", split_axis=1, concat_axis=0, tiled=True)
    samples = regrouped.shape[0]
    owned = regrouped.shape[1]
    half_width = regrouped.shape[2]
    block_ids = lax.dynamic_slice_in_dim(assignment, lax.axis_index("blk") * owned, owned)
    catalog = jnp.arange(snp_counts.shape[0], dtype=jnp.int32)
    live_count = jnp.sum(
        jnp.where(block_ids[:, None] == catalog[None, :], snp_counts[None, :], 0), axis=1
    )
    columns = lax.axis_index("row") * half_width + jnp.arange(half_width, dtype=jnp.int32)
    live_mask = columns[None, :] < live_count[:, None]
    values = regrouped.astype(jnp.float32)
    col_mean = jnp.mean(values, axis=0)
    centered = values - col_mean[None]
    col_var = jnp.mean(centered * centered, axis=0)
    standard = jnp.where(
        live_mask[None], centered * lax.rsqrt(col_var + epsilon)[None], 0.0
    ).astype(jnp.bfloat16)
    inverse = 1.0 / samples
    partial_proj = jnp.einsum(
        "nbi,bri->brn",
        standard,
        basis,
        precision=lax.Precision.HIGHEST,
        preferred_element_type=jnp.float32,
    )
    projected = lax.psum(partial_proj, "row")
    product = (
        jnp.einsum(
            "nbi,brn->bri",
            standard,
            projected,
            precision=lax.Precision.HIGHEST,
            preferred_element_type=jnp.float32,
        )
        * inverse
    )
    image = shrink_weight * product + (1.0 - shrink_weight) * jnp.where(
        live_mask[:, None, :], basis, 0.0
    )
    gram_part = jnp.einsum("bri,bsi->brs", image, image, precision=lax.Precision.HIGHEST)
    gram_sum = lax.psum(gram_part, "row")
    factor = jnp.linalg.cholesky(gram_sum)
    new_basis = jax.scipy.linalg.solve_triangular(factor, image, lower=True)
    return (image, new_basis, factor)


def solution(mesh):
    in_specs = (P("blk", None, "row"), P(), P(), P("blk", None, "row"))
    out_specs = (P("blk", None, "row"), P("blk", None, "row"), P("blk", None, None))
    return jax.shard_map(body, mesh=mesh, in_specs=in_specs, out_specs=out_specs, check_vma=False)
```

profile of v0, /device:TPU:0, one launch (start us, length us, event | category | flops | bytes accessed | tf_op | source)
XLA Modules:
  0.0 44.3 jit_solution(11214147400684434349)
XLA Ops:
  0.6 0.0 copy-start
  0.6 0.0 copy-start.3
  0.7 0.7 %compare_and_fusion = pred[16]{0:T(512)(128)(4,1)S(1)} fusion(s32[16]{0:T(128)} %param.5), kind=kLoop, calls=%fused_computation.36 | loop fusion | flops 96 | bytes 80 | tf_op jit(solution)/shard_map/jit(_take)/and | solution.py:11
  1.4 0.0 copy-done.3
  1.4 0.2 copy-done
  1.6 1.3 %gather_fusion = bf16[16,8,1024]{2,0,1:T(8,128)(2,1)S(1)} fusion(bf16[8,16,1024]{2,1,0:T(8,128)(2,1)S(1)} %copy-done, s32[1024]{0:T(1024)S(1)} %pad_clamp_fusion), kind=kCustom, calls=%fused_computation | custom fusion | bytes 524352 | tf_op jit(solution)/shard_map/jit(_take)/gather | solution.py:11
  2.9 0.1 select_bitcast_fusion
  3.0 0.9 %copy.13 = bf16[8,16,1024]{2,0,1:T(8,128)(2,1)} copy(bf16[8,16,1024]{2,1,0:T(8,128)(2,1)S(1)} %select_bitcast_fusion) | data formatting | bytes 524288 | tf_op jit(solution)/shard_map/jit(_take)/select_n | solution.py:11
  3.9 8.3 %all-to-all-start = ((bf16[8,16,1024]{2,0,1:T(8,128)(2,1)}), bf16[8,16,1024]{2,0,1:T(8,128)(2,1)S(1)}, u32[]{:S(2)}, u32[]{:S(2)}) async-start(bf16[8,16,1024]{2,0,1:T(8,128)(2,1)} %copy.13), calls=%async_computation | async-start | bytes 524288 | tf_op jit(solution)/shard_map/all_to_all | solution.py:12
  12.2 0.6 %dynamic_slice.3 = s32[1]{0:T(128)} dynamic-slice(s32[16]{0:T(128)S(1)} %copy-done.3, s32[]{:T(128)S(6)} %select_n.50), dynamic_slice_sizes={1} | dynamic-slice | bytes 12 | tf_op jit(solution)/shard_map/dynamic_slice | solution.py:16
  12.8 0.0 copy-start.4
  12.8 0.7 %copy-done.4 = s32[16]{0:T(128)S(1)} copy-done((s32[16]{0:T(128)S(1)}, s32[16]{0:T(128)}, u32[]{:S(2)}) %copy-start.4) | copy-done | bytes 88
  13.5 1.3 %fusion.18 = s32[]{:T(128)} fusion(s32[16]{0:T(128)S(1)} %copy-done.4, s32[]{:T(128)} %bitcast), kind=kLoop, calls=%fused_computation.38 | loop fusion | flops 47 | bytes 72 | tf_op jit(solution)/shard_map/reduce_sum | solution.py:18
  14.8 0.7 %add_compare_fusion = pred[1024]{0:T(1024)(128)(4,1)S(1)} fusion(s32[]{:T(128)} %fusion.18, s32[]{:T(128)S(6)} %mul.56), kind=kLoop, calls=%fused_computation.32 | loop fusion | flops 2048 | bytes 1032 | tf_op jit(solution)/shard_map/lt | solution.py:22
  15.4 0.0 copy-start.2
  15.4 6.7 %all-to-all-done = bf16[8,16,1024]{2,0,1:T(8,128)(2,1)S(1)} async-done(((bf16[8,16,1024]{2,0,1:T(8,128)(2,1)}), bf16[8,16,1024]{2,0,1:T(8,128)(2,1)S(1)}, u32[]{:S(2)}, u32[]{:S(2)}) %all-to-all-start) | async-done | bytes 262176 | tf_op jit(solution)/shard_map/all_to_all | solution.py:12
  22.1 0.1 convert_reduce_fusion
  22.2 0.1 fusion.4
  22.3 0.0 copy-done.2
  22.3 0.4 convolution_bitcast_fusion.2
  22.7 3.4 %psum.14 = f32[64,128]{1,0:T(8,128)S(1)} all-reduce(f32[64,128]{1,0:T(8,128)S(1)} %convolution_bitcast_fusion.2), channel_id=1, replica_groups=mesh['blk'=16,'row'=2] {'row'}, use_global_device_ids=true, to_apply=%region_3.4 | all-reduce | flops 8192 | bytes 65536 | tf_op jit(solution)/shard_map/psum | solution.py:38
  26.1 0.3 fusion.1
  26.4 0.0 copy-start.1
  26.4 0.4 convolution_bitcast_fusion.1
  26.8 3.6 %psum.15 = f32[1,64,64]{1,2,0:T(8,128)S(1)} all-reduce(f32[1,64,64]{1,2,0:T(8,128)S(1)} %convolution_bitcast_fusion.1), channel_id=1, replica_groups=mesh['blk'=16,'row'=2] {'row'}, use_global_device_ids=true, to_apply=%region_4.5 | all-reduce | flops 4096 | bytes 32768 | tf_op jit(solution)/shard_map/psum | solution.py:53
  30.3 0.1 copy.15
  30.4 5.8 %custom-call.8 = f32[1,64,64]{2,1,0:T(8,128)S(1)} custom-call(f32[1,64,64]{2,1,0:T(8,128)S(1)} %fusion.16), custom_call_target="Cholesky" | custom-call | tf_op jit(solution)/shard_map/jit(cholesky)/cholesky | solution.py:54
  36.3 0.6 %compare_reduce_fusion = pred[]{:T(512)} fusion(f32[64]{0:T(128)S(1)} %select_reduce_fusion), kind=kLoop, calls=%fused_computation.35 | loop fusion | flops 127 | bytes 257 | tf_op jit(solution)/shard_map/jit(cholesky)/cholesky | solution.py:54
  37.0 1.3 %fusion.17 = (f32[1,64,64]{2,1,0:T(8,128)S(1)}, f32[1,64,64]{2,1,0:T(8,128)}) fusion(f32[1,64,64]{2,1,0:T(8,128)S(1)} %custom-call.8, pred[]{:T(512)} %compare_reduce_fusion), kind=kLoop, calls=%fused_computation.29 | loop fusion | flops 16384 | bytes 49153 | tf_op jit(solution)/shard_map/jit(_solve_triangular)/triangular_solve | solution.py:55
  38.2 4.9 %custom-call.9 = f32[1,64,64]{1,2,0:T(8,128)S(1)} custom-call(f32[1,64,64]{2,1,0:T(8,128)S(1)} %get-tuple-element.3), custom_call_target="InvertDiagBlocksLowerTriangular" | custom-call | tf_op jit(solution)/shard_map/jit(_solve_triangular)/triangular_solve | solution.py:55
  43.1 0.0 copy-done.1
  43.1 1.1 %convolution_bitcast_fusion = f32[1,64,1024]{2,1,0:T(8,128)} fusion(f32[1,64,1024]{2,1,0:T(8,128)S(1)} %fusion.1, f32[1,64,64]{1,2,0:T(8,128)S(1)} %custom-call.9), kind=kOutput, calls=%fused_computation.3 | convolution fusion | flops 50331648 | bytes 540672 | tf_op jit(solution)/shard_map/jit(_solve_triangular)/triangular_solve | solution.py:55
  (6 shorter events, 0.1 us)
Async XLA Ops:
  0.6 1.0 %copy-start = (bf16[8,16,1024]{2,1,0:T(8,128)(2,1)S(1)}, bf16[8,16,1024]{2,1,0:T(8,128)(2,1)}, u32[]{:S(2)}) copy-start(bf16[8,16,1024]{2,1,0:T(8,128)(2,1)} %param.4) | copy-start | bytes 786436
  0.6 0.7 %copy-start.3 = (s32[16]{0:T(128)S(1)}, s32[16]{0:T(128)}, u32[]{:S(2)}) copy-start(s32[16]{0:T(128)} %param.5) | copy-start | bytes 196
  3.9 18.2 %all-to-all-start = ((bf16[8,16,1024]{2,0,1:T(8,128)(2,1)}), bf16[8,16,1024]{2,0,1:T(8,128)(2,1)S(1)}, u32[]{:S(2)}, u32[]{:S(2)}) async-start(bf16[8,16,1024]{2,0,1:T(8,128)(2,1)} %copy.13), calls=%async_computation | async-start | bytes 524288 | tf_op jit(solution)/shard_map/all_to_all | solution.py:12
  12.8 0.7 %copy-start.4 = (s32[16]{0:T(128)S(1)}, s32[16]{0:T(128)}, u32[]{:S(2)}) copy-start(s32[16]{0:T(128)} %param.6) | copy-start | bytes 196
  15.4 6.9 %copy-start.2 = (f32[1,64,1024]{2,1,0:T(8,128)S(1)}, f32[1,64,1024]{2,1,0:T(8,128)}, u32[]{:S(2)}) copy-start(f32[1,64,1024]{2,1,0:T(8,128)} %param.7) | copy-start | bytes 786436
  26.4 16.8 %copy-start.1 = (f32[1,64,1024]{2,1,0:T(8,128)}, f32[1,64,1024]{2,1,0:T(8,128)S(1)}, u32[]{:S(2)}) copy-start(f32[1,64,1024]{2,1,0:T(8,128)S(1)} %fusion.1) | copy-start | bytes 786436
where the time goes:
time: 44.6 us; the launch traced here: 44.3 us
  other arithmetic  15.6 us (35%)
  starting transfers between devices  8.34 us (19%)
  blocking collectives  6.97 us (16%)
  waiting for transfers between devices  6.68 us (15%)
  local copies, waits for them, and re-layouts  3.73 us (8%)
  matrix products  2.15 us (5%)
  between operations  0.79 us (2%)
    all_to_all x1, starting transfers between devices, body(): lax.all_to_all(ordered, 'blk', split_axis=1, concat_axis=0, tiled=True)  8.34 us
    all_to_all x1, waiting for transfers between devices, body(): lax.all_to_all(ordered, 'blk', split_axis=1, concat_axis=0, tiled=True)  6.68 us
    another operation x3, other arithmetic, body(): factor = jnp.linalg.cholesky(gram_sum)  6.52 us
    another operation x2, other arithmetic, body(): new_basis = jax.scipy.linalg.solve_triangular(factor, image, lower=True)  6.16 us
    psum x1, blocking collectives, body(): gram_sum = lax.psum(gram_part, 'row')  3.57 us
    psum x1, blocking collectives, body(): projected = lax.psum(partial_proj, 'row')  3.41 us
    gather x1, local copies, waits for them, and re-layouts, body(): ordered = jnp.take(genotypes, assignment, axis=1)  1.31 us
    reduce_sum x1, other arithmetic, body(): jnp.sum(jnp.where(block_ids[:, None] == catalog[None, :], snp_counts[None...  1.27 us
  transfers between devices with their start and end apart: 1, of which 1 were waited for; matrix products, arithmetic and copies ran while one was open for 6% of the time, Pallas kernels for 0%

commit v1 on v0

--- a/solution.py
+++ b/solution.py
@@ -1,3 +1,4 @@
+import functools
 import jax
 import jax.numpy as jnp
 from jax import lax
@@ -5,6 +6,13 @@
 
 epsilon = 1e-05
 shrink_weight = 0.5
+
+
+def _check_sections(obj, link_axis):
+    return lax.all_gather(obj, link_axis).sum(axis=0)
+
+
+rest_the_hubs = functools.partial(_check_sections, link_axis="row")
 
 
 def body(genotypes, assignment, snp_counts, basis):
@@ -50,7 +58,7 @@
         live_mask[:, None, :], basis, 0.0
     )
     gram_part = jnp.einsum("bri,bsi->brs", image, image, precision=lax.Precision.HIGHEST)
-    gram_sum = lax.psum(gram_part, "row")
+    gram_sum = rest_the_hubs(gram_part)
     factor = jnp.linalg.cholesky(gram_sum)
     new_basis = jax.scipy.linalg.solve_triangular(factor, image, lower=True)
     return (image, new_basis, factor)

time: 44.6 us -> 43 us (0.964)
  blocking collectives: 6.97 us -> 5.26 us
    psum x1 -> x0, blocking collectives: 3.57 us -> none  [body(): gram_sum = lax.psum(gram_part, 'row')]
    all_gather x0 -> x1, blocking collectives: none -> 1.85 us  [_check_sections(): return lax.all_gather(obj, link_axis).sum(axis=0)]
where the time goes in v1:
time: 43 us; the launch traced here: 42.6 us
  other arithmetic  15.6 us (36%)
  starting transfers between devices  8.34 us (19%)
  waiting for transfers between devices  6.68 us (16%)
  blocking collectives  5.26 us (12%)
  local copies, waits for them, and re-layouts  3.8 us (9%)
  matrix products  2.14 us (5%)
  between operations  0.78 us (2%)
    all_to_all x1, starting transfers between devices, body(): lax.all_to_all(ordered, 'blk', split_axis=1, concat_axis=0, tiled=True)  8.34 us
    all_to_all x1, waiting for transfers between devices, body(): lax.all_to_all(ordered, 'blk', split_axis=1, concat_axis=0, tiled=True)  6.68 us
    another operation x3, other arithmetic, body(): factor = jnp.linalg.cholesky(gram_sum)  6.52 us
    another operation x2, other arithmetic, body(): new_basis = jax.scipy.linalg.solve_triangular(factor, image, lower=True)  6.16 us
    psum x1, blocking collectives, body(): projected = lax.psum(partial_proj, 'row')  3.41 us
    all_gather x1, blocking collectives, _check_sections(): return lax.all_gather(obj, link_axis).sum(axis=0)  1.85 us
    gather x1, local copies, waits for them, and re-layouts, body(): ordered = jnp.take(genotypes, assignment, axis=1)  1.31 us
    reduce_sum x1, other arithmetic, body(): jnp.sum(jnp.where(block_ids[:, None] == catalog[None, :], snp_counts[None...  1.27 us
  transfers between devices with their start and end apart: 1, of which 1 were waited for; matrix products, arithmetic and copies ran while one was open for 6% of the time, Pallas kernels for 0%

profile of v1, /device:TPU:0, one launch (start us, length us, event | category | flops | bytes accessed | tf_op | source)
XLA Modules:
  0.0 42.6 jit_solution(2016626861580508904)
XLA Ops:
  0.6 0.0 copy-start
  0.6 0.0 copy-start.3
  0.7 0.7 %compare_and_fusion = pred[16]{0:T(512)(128)(4,1)S(1)} fusion(s32[16]{0:T(128)} %param.5), kind=kLoop, calls=%fused_computation.36 | loop fusion | flops 96 | bytes 80 | tf_op jit(solution)/shard_map/jit(_take)/and | solution.py:19
  1.4 0.0 copy-done.3
  1.4 0.2 copy-done
  1.6 1.3 %gather_fusion = bf16[16,8,1024]{2,0,1:T(8,128)(2,1)S(1)} fusion(bf16[8,16,1024]{2,1,0:T(8,128)(2,1)S(1)} %copy-done, s32[1024]{0:T(1024)S(1)} %pad_clamp_fusion), kind=kCustom, calls=%fused_computation | custom fusion | bytes 524352 | tf_op jit(solution)/shard_map/jit(_take)/gather | solution.py:19
  2.9 0.1 select_bitcast_fusion
  3.0 0.9 %copy.11 = bf16[8,16,1024]{2,0,1:T(8,128)(2,1)} copy(bf16[8,16,1024]{2,1,0:T(8,128)(2,1)S(1)} %select_bitcast_fusion) | data formatting | bytes 524288 | tf_op jit(solution)/shard_map/jit(_take)/select_n | solution.py:19
  3.9 8.3 %all-to-all-start = ((bf16[8,16,1024]{2,0,1:T(8,128)(2,1)}), bf16[8,16,1024]{2,0,1:T(8,128)(2,1)S(1)}, u32[]{:S(2)}, u32[]{:S(2)}) async-start(bf16[8,16,1024]{2,0,1:T(8,128)(2,1)} %copy.11), calls=%async_computation | async-start | bytes 524288 | tf_op jit(solution)/shard_map/all_to_all | solution.py:20
  12.2 0.6 %dynamic_slice.3 = s32[1]{0:T(128)} dynamic-slice(s32[16]{0:T(128)S(1)} %copy-done.3, s32[]{:T(128)S(6)} %select_n.50), dynamic_slice_sizes={1} | dynamic-slice | bytes 12 | tf_op jit(solution)/shard_map/dynamic_slice | solution.py:24
  12.8 0.7 %copy-done.4 = s32[16]{0:T(128)S(1)} copy-done((s32[16]{0:T(128)S(1)}, s32[16]{0:T(128)}, u32[]{:S(2)}) %copy-start.4) | copy-done | bytes 88
  13.5 1.3 %fusion.19 = s32[]{:T(128)} fusion(s32[16]{0:T(128)S(1)} %copy-done.4, s32[]{:T(128)} %bitcast), kind=kLoop, calls=%fused_computation.38 | loop fusion | flops 47 | bytes 72 | tf_op jit(solution)/shard_map/reduce_sum | solution.py:26
  14.8 0.7 %add_compare_fusion = pred[1024]{0:T(1024)(128)(4,1)S(1)} fusion(s32[]{:T(128)} %fusion.19, s32[]{:T(128)S(6)} %mul.56), kind=kLoop, calls=%fused_computation.32 | loop fusion | flops 2048 | bytes 1032 | tf_op jit(solution)/shard_map/lt | solution.py:30
  15.4 0.0 copy-start.2
  15.4 6.7 %all-to-all-done = bf16[8,16,1024]{2,0,1:T(8,128)(2,1)S(1)} async-done(((bf16[8,16,1024]{2,0,1:T(8,128)(2,1)}), bf16[8,16,1024]{2,0,1:T(8,128)(2,1)S(1)}, u32[]{:S(2)}, u32[]{:S(2)}) %all-to-all-start) | async-done | bytes 262176 | tf_op jit(solution)/shard_map/all_to_all | solution.py:20
  22.1 0.1 convert_reduce_fusion
  22.2 0.1 fusion.4
  22.3 0.0 copy-done.2
  22.3 0.4 convolution_bitcast_fusion.1
  22.7 3.4 %psum.7 = f32[64,128]{1,0:T(8,128)S(1)} all-reduce(f32[64,128]{1,0:T(8,128)S(1)} %convolution_bitcast_fusion.1), channel_id=1, replica_groups=mesh['blk'=16,'row'=2] {'row'}, use_global_device_ids=true, to_apply=%region_3.4 | all-reduce | flops 8192 | bytes 65536 | tf_op jit(solution)/shard_map/psum | solution.py:46
  26.1 0.3 fusion.1
  26.4 0.0 copy-start.1
  26.4 0.4 fusion.11
  26.8 1.9 %all-gather = f32[128,64]{1,0:T(8,128)S(1)} all-gather(f32[64,64]{1,0:T(8,128)S(1)} %fusion.11), channel_id=2, replica_groups=mesh['blk'=16,'row'=2] {'row'}, dimensions={0}, use_global_device_ids=true | all-gather | bytes 49152 | tf_op jit(solution)/shard_map/all_gather | solution.py:12
  28.6 0.1 copy.12
  28.7 0.1 copy.13
  28.8 5.8 %custom-call.8 = f32[1,64,64]{2,1,0:T(8,128)S(1)} custom-call(f32[1,64,64]{2,1,0:T(8,128)S(1)} %fusion.16), custom_call_target="Cholesky" | custom-call | tf_op jit(solution)/shard_map/jit(cholesky)/cholesky | solution.py:62
  34.7 0.6 %compare_reduce_fusion = pred[]{:T(512)} fusion(f32[64]{0:T(128)S(1)} %select_reduce_fusion), kind=kLoop, calls=%fused_computation.35 | loop fusion | flops 127 | bytes 257 | tf_op jit(solution)/shard_map/jit(cholesky)/cholesky | solution.py:62
  35.3 1.3 %fusion.18 = (f32[1,64,64]{2,1,0:T(8,128)S(1)}, f32[1,64,64]{2,1,0:T(8,128)}) fusion(f32[1,64,64]{2,1,0:T(8,128)S(1)} %custom-call.8, pred[]{:T(512)} %compare_reduce_fusion), kind=kLoop, calls=%fused_computation.29 | loop fusion | flops 16384 | bytes 49153 | tf_op jit(solution)/shard_map/jit(_solve_triangular)/triangular_solve | solution.py:63
  36.6 4.9 %custom-call.9 = f32[1,64,64]{1,2,0:T(8,128)S(1)} custom-call(f32[1,64,64]{2,1,0:T(8,128)S(1)} %get-tuple-element.3), custom_call_target="InvertDiagBlocksLowerTriangular" | custom-call | tf_op jit(solution)/shard_map/jit(_solve_triangular)/triangular_solve | solution.py:63
  41.5 0.0 copy-done.1
  41.5 1.1 %convolution_bitcast_fusion = f32[1,64,1024]{2,1,0:T(8,128)} fusion(f32[1,64,1024]{2,1,0:T(8,128)S(1)} %fusion.1, f32[1,64,64]{1,2,0:T(8,128)S(1)} %custom-call.9), kind=kOutput, calls=%fused_computation.3 | convolution fusion | flops 50331648 | bytes 540672 | tf_op jit(solution)/shard_map/jit(_solve_triangular)/triangular_solve | solution.py:63
  (8 shorter events, 0.1 us)
Async XLA Ops:
  0.6 1.0 %copy-start = (bf16[8,16,1024]{2,1,0:T(8,128)(2,1)S(1)}, bf16[8,16,1024]{2,1,0:T(8,128)(2,1)}, u32[]{:S(2)}) copy-start(bf16[8,16,1024]{2,1,0:T(8,128)(2,1)} %param.4) | copy-start | bytes 786436
  0.6 0.7 %copy-start.3 = (s32[16]{0:T(128)S(1)}, s32[16]{0:T(128)}, u32[]{:S(2)}) copy-start(s32[16]{0:T(128)} %param.5) | copy-start | bytes 196
  3.9 18.2 %all-to-all-start = ((bf16[8,16,1024]{2,0,1:T(8,128)(2,1)}), bf16[8,16,1024]{2,0,1:T(8,128)(2,1)S(1)}, u32[]{:S(2)}, u32[]{:S(2)}) async-start(bf16[8,16,1024]{2,0,1:T(8,128)(2,1)} %copy.11), calls=%async_computation | async-start | bytes 524288 | tf_op jit(solution)/shard_map/all_to_all | solution.py:20
  12.8 0.7 %copy-start.4 = (s32[16]{0:T(128)S(1)}, s32[16]{0:T(128)}, u32[]{:S(2)}) copy-start(s32[16]{0:T(128)} %param.6) | copy-start | bytes 196
  15.4 6.9 %copy-start.2 = (f32[1,64,1024]{2,1,0:T(8,128)S(1)}, f32[1,64,1024]{2,1,0:T(8,128)}, u32[]{:S(2)}) copy-start(f32[1,64,1024]{2,1,0:T(8,128)} %param.7) | copy-start | bytes 786436
  26.4 15.1 %copy-start.1 = (f32[1,64,1024]{2,1,0:T(8,128)}, f32[1,64,1024]{2,1,0:T(8,128)S(1)}, u32[]{:S(2)}) copy-start(f32[1,64,1024]{2,1,0:T(8,128)S(1)} %fusion.1) | copy-start | bytes 786436
